TPU v7x, 32 devices: a 4x4x1 block of a 4x4x8 slice. The times are simulated.
32 devices in a mesh: rep: 2 (over z, core), dp: 16 (over x, y).
Axes of the slice: x: 4, y: 4, z: 1, core: 2. Of those that a mesh axis runs over, the one named last changes fastest.
The devices are a block of a 4x4x8 slice.
Arguments:
- x: bfloat16 [32, 2048, 640], P(('rep', 'dp')), parts along dimension 0
- dy: bfloat16 [32, 2048, 640], P(('rep', 'dp')), parts along dimension 0
- w_gate: bfloat16 [2, 640, 2048], replicated
- w_up: bfloat16 [2, 640, 2048], replicated
- w_down: bfloat16 [2, 2048, 640], replicated
- m_w_gate: float32 [2, 640, 2048], P(None, 'dp')
- m_w_up: float32 [2, 640, 2048], P(None, 'dp')
- m_w_down: float32 [2, 2048, 640], P(None, 'dp')
- v_w_gate: float32 [2, 640, 2048], P(None, 'dp')
- v_w_up: float32 [2, 640, 2048], P(None, 'dp')
- v_w_down: float32 [2, 2048, 640], P(None, 'dp')
Outputs:
- output 1: bfloat16 [4, 640, 2048], P('rep'), parts along dimension 0
- output 2: bfloat16 [4, 640, 2048], P('rep'), parts along dimension 0
- output 3: bfloat16 [4, 2048, 640], P('rep'), parts along dimension 0
- output 4: float32 [4, 640, 2048], P('rep', 'dp'), parts along dimension 0
- output 5: float32 [4, 640, 2048], P('rep', 'dp'), parts along dimension 0
- output 6: float32 [4, 2048, 640], P('rep', 'dp'), parts along dimension 0
- output 7: float32 [4, 640, 2048], P('rep', 'dp'), parts along dimension 0
- output 8: float32 [4, 640, 2048], P('rep', 'dp'), parts along dimension 0
- output 9: float32 [4, 2048, 640], P('rep', 'dp'), parts along dimension 0
There are 2 independent parts. A program takes and returns all parts, laid end to end along the dimension named above; an argument that names none is the same for every part.
All inputs are finite; a program needn't handle non-finite values.
Results may differ from a plain program's by a relative error of at most 0.022.
Values are sent between devices in bfloat16 or wider.
A program may use at most 768 MiB of HBM per device.

v0:
```python
import functools
import math

import jax
import jax.numpy as jnp
from jax import lax
from jax.experimental import pallas as pl
from jax.experimental.pallas import tpu as pltpu
from jax.sharding import PartitionSpec as P

BF, F32 = jnp.bfloat16, jnp.float32
MESH = pl.DeviceIdType.MESH
ANY = pl.BlockSpec(memory_space=pl.ANY)
VMEM_LIMIT = 66 * 1024 * 1024 - 2 * 1024 * 1024

UNITS = (("d", 1), ("g", 1), ("u", 1), ("d", 0), ("g", 0), ("u", 0))
WIDE = (("g", 1), ("u", 1), ("g", 0), ("u", 0))
TALL = (("d", 1), ("d", 0))
BLOCKS = 4
TOKEN_BLOCKS = 4


def adamw(w, m, v, g):
    m = 0.9 * m + 0.1 * g
    v = 0.95 * v + 0.05 * g * g
    step = m * lax.rsqrt(v + 1e-8) + 0.1 * w
    return (w - 0.02 * step).astype(BF), m, v


def step_kernel(side, rows, cols, *refs):
    dy_t, a1_t, a0_t = refs[0:3]
    act1, dg1, du1, act0, p0, s0, h1, dy, gate1, up1, down0 = refs[3:14]
    gate1, up1, down0 = gate1.at[1], up1.at[1], down0.at[0]
    w_in, m_in, v_in = refs[14:17], refs[17:20], refs[20:23]
    w_out, m_out, v_out, (dg0, du0) = refs[23:26], refs[26:29], refs[29:32], refs[32:34]
    (gw, gt, r1w, r1t, r2w, r2t, left_buf, right_buf, dh_t, down_buf, h_buf, factor_buf, out_buf, ow, ot, mw, mt, vw, vt, g_full) = refs[34:54]
    (send1, recv1, send2, recv2, left_sem, right_sem, tile_sem, h_sem, factor_sem, tile_out_sem, state_sem, out_sem) = refs[54:]
    rights = {("d", 1): act1, ("g", 1): dg1, ("u", 1): du1, ("d", 0): act0, ("g", 0): dg0, ("u", 0): du0}
    me = lax.axis_index("dp")
    at = (me // side, me % side)
    kinds = ("g", "u", "d")

    def index(x, y):
        return lax.rem(x + side, side) * side + lax.rem(y + side, side)

    def near(axis, by):
        return index(at[0] + by, at[1]) if axis == 0 else index(at[0], at[1] + by)

    steps = {(axis, by): lax.rem(at[axis] + by + side, side) for axis in (0, 1) for by in (-1, 1, 2)}

    def along(axis, by):
        return steps[axis, by]

    right_of, left_of = [near(a, 1) for a in (0, 1)], [near(a, -1) for a in (0, 1)]

    def part(unit, h, s):
        if unit[0] == "d":
            size = g_full.shape[0] // 4
            return (pl.ds((2 * h + s) * size, size), slice(None))
        size = gw.shape[-1] // 4
        return (slice(None), pl.ds((2 * h + s) * size, size))

    def pick(unit):
        if unit[0] == "d":
            n = TALL.index(unit)
            return gt.at[n], r1t.at[n], r2t.at[n]
        n = WIDE.index(unit)
        return gw.at[n], r1w.at[n], r2w.at[n]

    def several(unit, h, i, s):
        g = pick(unit)[0]
        lead = (i, slice(None)) if h == 0 else (slice(None), i)
        return g.at[lead + part(unit, h, s)]

    def single(unit, h, i, j, s):
        g = pick(unit)[0]
        lead = (i, j) if h == 0 else (j, i)
        return g.at[lead + part(unit, h, s)]

    def remote(src, dst, send, recv, to):
        return pltpu.make_async_remote_copy(src_ref=src, dst_ref=dst, send_sem=send, recv_sem=recv, device_id={"dp": to}, device_id_type=MESH)

    sent = []

    def push(src, dst, send, recv, to):
        remote(src(), dst(), send(), recv(), to).start()
        sent.append((src, dst, send, recv, to))

    def arrived(dst, send, recv):
        remote(dst, dst, send, recv, right_of[0]).wait_recv()

    def push1(unit, h, slot, src, dst, to):
        u = UNITS.index(unit)
        push(src, dst, lambda: send1.at[u, h, slot], lambda: recv1.at[u, h, slot], to)

    def push2(unit, h, slot, src, dst, to):
        u = UNITS.index(unit)
        push(src, dst, lambda: send2.at[u, h, slot], lambda: recv2.at[u, h, slot], to)

    def arrived1(unit, h, slot):
        u = UNITS.index(unit)
        dst = pick(unit)[1].at[h, slot] if slot < 6 else pick(unit)[2].at[h, slot - 6]
        arrived(dst, send1.at[u, h, slot], recv1.at[u, h, slot])

    def first(unit, h, slot):
        return lambda: pick(unit)[1].at[h, slot]

    def second(unit, h, slot):
        return lambda: pick(unit)[2].at[h, slot]

    def phase1_send(unit):
        for h in (0, 1):
            far, nxt, prv = along(h, 2), along(h, 1), along(h, -1)
            for slot, i, s, to in ((0, far, 1, right_of[h]), (1, far, 0, left_of[h]), (2, nxt, 0, right_of[h]), (3, prv, 1, left_of[h])):
                push1(unit, h, slot, functools.partial(several, unit, h, i, s), first(unit, h, slot), to)

    def phase1_pass(unit):
        r1 = pick(unit)[1]
        for h in (0, 1):
            for slot, i, s, out, to in ((0, along(h, 1), 1, 4, right_of[h]), (1, along(h, -1), 0, 5, left_of[h])):
                arrived1(unit, h, slot)
                for j in range(side):
                    here = single(unit, h, i, j, s)
                    here[...] = (here[...].astype(F32) + r1[h, slot, j].astype(F32)).astype(BF)
                push1(unit, h, out, functools.partial(several, unit, h, i, s), first(unit, h, out), to)

    def row_sum(unit, h, j, s):
        _, r1, _ = pick(unit)
        one, two = (2, 5) if s == 0 else (4, 3)
        return single(unit, h, at[h], j, s)[...].astype(F32) + r1[h, one, j].astype(F32) + r1[h, two, j].astype(F32)

    def phase2_send(unit):
        for h in (0, 1):
            for slot in (2, 3, 4, 5):
                arrived1(unit, h, slot)
            o = 1 - h
            far, nxt, prv = along(o, 2), along(o, 1), along(o, -1)
            for slot, j, s, to in ((0, far, 1, right_of[o]), (1, far, 0, left_of[o]), (2, nxt, 0, right_of[o]), (3, prv, 1, left_of[o])):
                single(unit, h, at[h], j, s)[...] = row_sum(unit, h, j, s).astype(BF)
                push1(unit, h, 6 + slot, functools.partial(single, unit, h, at[h], j, s), second(unit, h, slot), to)

    def phase2_pass(unit):
        r2 = pick(unit)[2]
        for h in (0, 1):
            o = 1 - h
            for slot, j, s, out, to in ((0, along(o, 1), 1, 4, right_of[o]), (1, along(o, -1), 0, 5, left_of[o])):
                arrived1(unit, h, 6 + slot)
                single(unit, h, at[h], j, s)[...] = (row_sum(unit, h, j, s) + r2[h, slot].astype(F32)).astype(BF)
                push1(unit, h, 6 + out, functools.partial(single, unit, h, at[h], j, s), second(unit, h, out), to)

    def state(unit):
        k = kinds.index(unit[0])
        n = TALL.index(unit) if unit[0] == "d" else WIDE.index(unit)
        own, m, v = (ot, mt, vt) if unit[0] == "d" else (ow, mw, vw)
        return k, own.at[n], m.at[n], v.at[n]

    def state_copies(unit, which=(0, 1, 2)):
        u = UNITS.index(unit)
        k, own, m, v = state(unit)
        layer = unit[1]
        pairs = ((w_in[k].at[layer, me], own), (m_in[k].at[layer], m), (v_in[k].at[layer], v))
        return [pltpu.make_async_copy(*pairs[i], state_sem.at[u, i]) for i in which]

    def result_copies(unit, which=(0, 1, 2)):
        u = UNITS.index(unit)
        k, own, m, v = state(unit)
        layer = unit[1]
        pairs = ((own, w_out[k].at[layer, at[0], at[1]]), (m, m_out[k].at[layer]), (v, v_out[k].at[layer]))
        return [pltpu.make_async_copy(*pairs[i], out_sem.at[u, i]) for i in which]

    def total(unit, h, s):
        _, _, r2 = pick(unit)
        one, two = (2, 5) if s == 0 else (4, 3)
        g = row_sum(unit, h, at[1 - h], s) + r2[h, one].astype(F32) + r2[h, two].astype(F32)
        return g.astype(BF).astype(F32)

    def w_part(unit, h, s):
        k, own, _, _ = state(unit)
        if unit[0] == "d":
            size = own.shape[0] // 4
            start, count = ((2 * h + s) * size, size) if s is not None else (2 * h * size, 2 * size)
            return (pl.ds(start, count), slice(None))
        size = own.shape[1] // 4
        start, count = ((2 * h + s) * size, size) if s is not None else (2 * h * size, 2 * size)
        return (slice(None), pl.ds(start, count))

    def w_single(unit, h, i, j, s):
        k = kinds.index(unit[0])
        lead = (i, j) if h == 0 else (j, i)
        return w_out[k].at[(unit[1],) + lead + w_part(unit, h, s)]

    def w_several(unit, h, i, s):
        k = kinds.index(unit[0])
        lead = (i, slice(None)) if h == 0 else (slice(None), i)
        return w_out[k].at[(unit[1],) + lead + w_part(unit, h, s)]

    def update(unit):
        u = UNITS.index(unit)
        k, own, m, v = state(unit)
        for copy in state_copies(unit):
            copy.wait()
        for h in (0, 1):
            for slot in (2, 3, 4, 5):
                arrived1(unit, h, 6 + slot)
        if unit[0] == "d":
            for h in (0, 1):
                for s in (0, 1):
                    g_full[part(unit, h, s)[0], :] = total(unit, h, s)
            own[...], m[...], v[...] = adamw(own[...].astype(F32), m[...], v[...], g_full[...].T)
        else:
            for h in (0, 1):
                for s in (0, 1):
                    c = part(unit, h, s)
                    own[c], m[c], v[c] = adamw(own[c].astype(F32), m[c], v[c], total(unit, h, s))
        for copy in result_copies(unit):
            copy.start()
        for h in (0, 1):
            o = 1 - h
            src = lambda unit=unit, h=h: state(unit)[1].at[w_part(unit, h, None)]
            dst = functools.partial(w_single, unit, h, at[h], at[o], None)
            push2(unit, h, 0, src, dst, right_of[o])
            push2(unit, h, 1, src, dst, left_of[o])

    def arrived2(unit, h, slot, dst):
        u = UNITS.index(unit)
        arrived(dst, send2.at[u, h, slot], recv2.at[u, h, slot])

    def gather1_pass(unit):
        for h in (0, 1):
            o = 1 - h
            for slot, by, s, to in ((0, -1, 1, right_of[o]), (1, 1, 0, left_of[o])):
                arrived2(unit, h, slot, w_single(unit, h, at[h], along(o, by), None))
                piece = functools.partial(w_single, unit, h, at[h], along(o, by), s)
                push2(unit, h, 2 + slot, piece, piece, to)

    def gather2_send(unit):
        result_copies(unit, (0,))[0].wait()
        for h in (0, 1):
            o = 1 - h
            for slot, s in ((2, 1), (3, 0)):
                arrived2(unit, h, slot, w_single(unit, h, at[h], along(o, 2), s))
            piece = functools.partial(w_several, unit, h, at[h], None)
            push2(unit, h, 4, piece, piece, right_of[h])
            push2(unit, h, 5, piece, piece, left_of[h])

    def gather2_pass(unit):
        for h in (0, 1):
            for slot, by, s, to in ((4, -1, 1, right_of[h]), (5, 1, 0, left_of[h])):
                arrived2(unit, h, slot, w_several(unit, h, along(h, by), None))
                piece = functools.partial(w_several, unit, h, along(h, by), s)
                push2(unit, h, 2 + slot, piece, piece, to)

    def gather2_end(unit):
        for h in (0, 1):
            for slot, s in ((6, 1), (7, 0)):
                arrived2(unit, h, slot, w_several(unit, h, along(h, 2), s))

    width = right_buf.shape[-1]
    count = right_buf.shape[1]

    def fill(src, slot):
        return pltpu.make_async_copy(src, left_buf.at[slot], left_sem.at[slot])

    def right_copy(unit, n, slot):
        columns = pl.ds(pl.multiple_of(n * width, width), width)
        return pltpu.make_async_copy(rights[unit].at[:, :, columns], right_buf_of(slot), right_sem.at[slot])

    def right_buf_of(slot):
        return right_buf.at[pl.ds(slot * TOKEN_BLOCKS, TOKEN_BLOCKS)]

    def gradient(unit, left, then):
        def block(n, _):
            slot = lax.rem(n, 2)

            @pl.when(n < BLOCKS - 1)
            def _():
                right_copy(unit, n + 1, 1 - slot).start()

            if then is not None:

                @pl.when(n == BLOCKS - 1)
                def _():
                    right_copy(then, 0, 1 - slot).start()

            right_copy(unit, n, slot).wait()
            right = right_buf[pl.ds(slot * TOKEN_BLOCKS, TOKEN_BLOCKS)].reshape(TOKEN_BLOCKS * count, width)
            out = jnp.dot(left[...], right, preferred_element_type=F32)
            g = pick(unit)[0]
            if unit[0] == "d":
                for c in range(width // cols):
                    chunk = n * (width // cols) + c
                    g[chunk // side, lax.rem(chunk, side)] = out[:, c * cols : (c + 1) * cols].astype(BF)
            else:
                for x in range(side):
                    for y in range(side):
                        r = (x * side + y) * rows
                        g[x, y, :, pl.ds(pl.multiple_of(n * width, width), width)] = out[r : r + rows].astype(BF)
            return 0

        lax.fori_loop(0, BLOCKS, block, 0)

    def tile(src, t, f, slot):
        return pltpu.make_async_copy(src.at[t, :, pl.ds(f * width, width)], right_buf.at[slot * TOKEN_BLOCKS + f], tile_sem.at[slot, f])

    def tiles(src, t, slot):
        return [tile(src, t, f, slot) for f in range(BLOCKS)]

    def state_tiles(t):
        return [pltpu.make_async_copy(src.at[t], h_buf.at[i], h_sem.at[i]) for i, src in enumerate((h1, dy))]

    def factor_tiles(t, f, slot):
        return [pltpu.make_async_copy(src.at[t, :, pl.ds(f * width, width)], factor_buf.at[slot, i], factor_sem.at[slot, i]) for i, src in enumerate((p0, s0))]

    def result_tiles(t, f, slot):
        return [pltpu.make_async_copy(out_buf.at[slot, i], dst.at[t, :, pl.ds(f * width, width)], tile_out_sem.at[slot, i]) for i, dst in enumerate((dg0, du0))]

    def start(copies):
        for copy in copies:
            copy.start()

    def wait(copies):
        for copy in copies:
            copy.wait()

    def against(buf, slot):
        total = None
        for f in range(BLOCKS):
            term = lax.dot_general(right_buf[slot * TOKEN_BLOCKS + f], buf[:, f * width : (f + 1) * width], (((1,), (1,)), ((), ())), preferred_element_type=F32)
            total = term if total is None else total + term
        return total.astype(BF).astype(F32)

    def between(work):
        start(tiles(du1, 0, 1))
        down = pltpu.make_async_copy(down0, down_buf, left_sem.at[2])

        def block(t, _):
            last = TOKEN_BLOCKS - 1
            start(factor_tiles(t, 0, 0))
            wait(tiles(dg1, t, 0))
            da = against(left_buf.at[0], 0)

            @pl.when(t < last)
            def _():
                start(tiles(dg1, t + 1, 0))

            wait(tiles(du1, t, 1))
            da = da + against(left_buf.at[1], 1)

            @pl.when(t < last)
            def _():
                start(tiles(du1, t + 1, 1))

            wait(state_tiles(t))
            h = h_buf[0].astype(F32)
            da = da.astype(BF).astype(F32)
            scale = lax.rsqrt(jnp.mean(h * h, -1, keepdims=True) + 1e-6)
            inner = jnp.sum(da * h, -1, keepdims=True)
            back = da * scale - h * (scale * scale * scale * inner / h.shape[-1])
            dh = h_buf[1].astype(F32) + back.astype(BF).astype(F32)
            dh_t[:, pl.ds(pl.multiple_of(t * count, count), count)] = dh.T.astype(BF)
            dh = dh.astype(BF)

            @pl.when(t < last)
            def _():
                start(state_tiles(t + 1))

            for f in range(BLOCKS):
                slot = f % 2
                if f + 1 < BLOCKS:
                    start(factor_tiles(t, f + 1, 1 - slot))
                d = lax.dot_general(dh, down_buf[f * width : (f + 1) * width], (((1,), (1,)), ((), ())), preferred_element_type=F32).astype(BF).astype(F32)
                wait(factor_tiles(t, f, slot))
                if f >= 2:
                    wait(result_tiles(t, f - 2, slot))
                for i in (0, 1):
                    out_buf[slot, i] = (d * factor_buf[slot, i]).astype(BF)
                start(result_tiles(t, f, slot))
            for f in (BLOCKS - 2, BLOCKS - 1):
                wait(result_tiles(t, f, f % 2))
            for k in range(TOKEN_BLOCKS):

                @pl.when(t == k)
                def _():
                    work(k)

            return 0

        wait([fill(gate1, 0), fill(up1, 1), down])
        lax.fori_loop(0, TOKEN_BLOCKS, block, 0)

    start([fill(dy_t, 0), right_copy(UNITS[0], 0, 0), fill(a1_t, 1), pltpu.make_async_copy(down0, down_buf, left_sem.at[2])])
    start(state_tiles(0))
    for unit in UNITS:
        start(state_copies(unit))
    barrier = pltpu.get_barrier_semaphore()
    for a in (0, 1):
        for to in (left_of[a], right_of[a]):
            pl.semaphore_signal(barrier, inc=1, device_id={"dp": to}, device_id_type=MESH)
    pl.semaphore_wait(barrier, 4)

    stages = (phase1_send, phase1_pass, phase2_send, phase2_pass, update, gather1_pass, gather2_send, gather2_pass, gather2_end)
    begins = dict(zip(UNITS, (0, 1, 2, 3 + TOKEN_BLOCKS, 4 + TOKEN_BLOCKS, 5 + TOKEN_BLOCKS), strict=True))

    def communicate(t):
        for unit in UNITS:
            if 0 <= t - begins[unit] < len(stages):
                stages[t - begins[unit]](unit)

    d1, g1, u1, d0, g0, u0 = UNITS
    fill(dy_t, 0).wait()
    gradient(d1, left_buf.at[0], g1)
    fill(gate1, 0).start()
    communicate(0)
    fill(a1_t, 1).wait()
    gradient(g1, left_buf.at[1], u1)
    communicate(1)
    gradient(u1, left_buf.at[1], None)
    fill(up1, 1).start()
    start(tiles(dg1, 0, 0))
    communicate(2)
    between(lambda k: communicate(3 + k))
    fill(a0_t, 0).start()
    right_copy(d0, 0, 0).start()
    gradient(d0, dh_t, g0)
    communicate(begins[d0])
    fill(a0_t, 0).wait()
    gradient(g0, left_buf.at[0], u0)
    communicate(begins[g0])
    gradient(u0, left_buf.at[0], None)
    for t in range(begins[u0], begins[u0] + len(stages)):
        communicate(t)
    for unit in UNITS:
        wait(result_copies(unit, (1, 2)))
    for src, dst, send, recv, to in sent:
        remote(src(), dst(), send(), recv(), to).wait_send()


def reduce_step_gather(n, dy_t, a1_t, a0_t, act1, dg1, du1, act0, p0, s0, h1, dy, weights, m, v):
    side = math.isqrt(n)
    layers, rows, ff = m[0].shape
    cols, d = m[2].shape[1:]
    blocked = [w.reshape(layers, n, -1, w.shape[-1]) for w in weights]
    half, part = ff // 2, ff // 4
    width = ff // BLOCKS
    tokens = dy_t.shape[1]
    count = tokens // TOKEN_BLOCKS
    tiled = [t.reshape(TOKEN_BLOCKS, count, t.shape[-1]) for t in (act1, dg1, du1, act0, p0, s0, h1, dy)]
    out_shape = (
        [jax.ShapeDtypeStruct((layers, side, side, rows, ff), BF)] * 2
        + [jax.ShapeDtypeStruct((layers, side, side, cols, d), BF)]
        + [jax.ShapeDtypeStruct(t.shape, F32) for t in (*m, *v)]
        + [jax.ShapeDtypeStruct((TOKEN_BLOCKS, count, ff), BF)] * 2
    )
    nw, nt, nu = len(WIDE), len(TALL), len(UNITS)
    dma = pltpu.SemaphoreType.DMA
    out = pl.pallas_call(
        functools.partial(step_kernel, side, rows, cols),
        out_shape=out_shape,
        in_specs=[ANY] * 23,
        out_specs=[ANY] * 11,
        scratch_shapes=[
            pltpu.VMEM((nw, side, side, rows, ff), BF),
            pltpu.VMEM((nt, side, side, d, cols), BF),
            pltpu.VMEM((nw, 2, 6, side, rows, part), BF),
            pltpu.VMEM((nt, 2, 6, side, d // 4, cols), BF),
            pltpu.VMEM((nw, 2, 6, rows, part), BF),
            pltpu.VMEM((nt, 2, 6, d // 4, cols), BF),
            pltpu.VMEM((2, d, tokens), BF),
            pltpu.VMEM((2 * TOKEN_BLOCKS, count, width), BF),
            pltpu.VMEM((d, tokens), BF),
            pltpu.VMEM((ff, d), BF),
            pltpu.VMEM((2, count, d), BF),
            pltpu.VMEM((2, 2, count, width), F32),
            pltpu.VMEM((2, 2, count, width), BF),
            pltpu.VMEM((nw, rows, ff), BF),
            pltpu.VMEM((nt, cols, d), BF),
            pltpu.VMEM((nw, rows, ff), F32),
            pltpu.VMEM((nt, cols, d), F32),
            pltpu.VMEM((nw, rows, ff), F32),
            pltpu.VMEM((nt, cols, d), F32),
            pltpu.VMEM((d, cols), F32),
            dma((nu, 2, 12)),
            dma((nu, 2, 12)),
            dma((nu, 2, 8)),
            dma((nu, 2, 8)),
            dma((3,)),
            dma((2,)),
            dma((2, BLOCKS)),
            dma((2,)),
            dma((2, 2)),
            dma((2, 2)),
            dma((nu, 3)),
            dma((nu, 3)),
        ],
        compiler_params=pltpu.CompilerParams(collective_id=0, has_side_effects=True, vmem_limit_bytes=VMEM_LIMIT),
        name="reduce_step_gather",
    )(dy_t, a1_t, a0_t, *tiled, *weights, *blocked, *m, *v)
    return tuple(w.reshape(layers, -1, w.shape[-1]) for w in out[:3]) + tuple(out[3:9])


def front_kernel(x, dy, *refs):
    weights, (act0, act1, dg1, du1, p0, s0, h1, a0_t, a1_t, dy_t), bufs, a_buf, sem = refs[:3], refs[3:13], refs[13:16], refs[16], refs[17]
    first = pl.program_id(0) == 0
    ff = act0.shape[1]
    width = ff // BLOCKS

    def copy(layer, k):
        return pltpu.make_async_copy(weights[k].at[layer], bufs[k].at[layer], sem.at[layer, k])

    def normed(h, t_ref):
        wide = h[...].astype(F32)
        a = wide * lax.rsqrt(jnp.mean(wide * wide, -1, keepdims=True) + 1e-6)
        a_buf[...] = a.astype(BF)
        t_ref[...] = a.T.astype(BF)

    @pl.when(first)
    def _():
        for layer in (0, 1):
            for k in range(3):
                copy(layer, k).start()

    normed(x, a0_t)
    dy_t[...] = dy[...].astype(F32).T.astype(BF)

    def ready(layer):
        @pl.when(first)
        def _():
            for k in range(3):
                copy(layer, k).wait()

    ready(0)
    for f in range(BLOCKS):
        c = slice(f * width, (f + 1) * width)
        gate = jnp.dot(a_buf[...], bufs[0][0, :, c], preferred_element_type=F32)
        up = jnp.dot(a_buf[...], bufs[1][0, :, c], preferred_element_type=F32)
        sig = jax.nn.sigmoid(gate)
        silu = gate * sig
        act0[:, c] = (silu * up).astype(BF)
        p0[:, c] = up * (sig + silu * (1 - sig))
        s0[:, c] = silu
    h1[...] = (x[...].astype(F32) + jnp.dot(act0[...], bufs[2][0], preferred_element_type=F32).astype(BF).astype(F32)).astype(BF)
    normed(h1, a1_t)
    ready(1)
    for f in range(BLOCKS):
        c = slice(f * width, (f + 1) * width)
        gate = jnp.dot(a_buf[...], bufs[0][1, :, c], preferred_element_type=F32)
        up = jnp.dot(a_buf[...], bufs[1][1, :, c], preferred_element_type=F32)
        d = lax.dot_general(dy[...], bufs[2][1, c, :], (((1,), (1,)), ((), ())), preferred_element_type=F32).astype(BF).astype(F32)
        sig = jax.nn.sigmoid(gate)
        silu = gate * sig
        act1[:, c] = (silu * up).astype(BF)
        dg1[:, c] = (d * up * (sig + silu * (1 - sig))).astype(BF)
        du1[:, c] = (d * silu).astype(BF)


def front(x, dy, weights):
    tokens, d = x.shape
    layers, _, ff = weights[0].shape
    count = tokens // TOKEN_BLOCKS
    row = lambda n: pl.BlockSpec((count, n), lambda t: (t, 0))
    column = pl.BlockSpec((d, count), lambda t: (0, t))
    shape = jax.ShapeDtypeStruct
    return pl.pallas_call(
        front_kernel,
        grid=(TOKEN_BLOCKS,),
        out_shape=[shape((tokens, ff), BF)] * 4 + [shape((tokens, ff), F32)] * 2 + [shape((tokens, d), BF)] + [shape((d, tokens), BF)] * 3,
        in_specs=[row(d)] * 2 + [ANY] * 3,
        out_specs=[row(ff)] * 6 + [row(d)] + [column] * 3,
        scratch_shapes=[pltpu.VMEM(w.shape, BF) for w in weights] + [pltpu.VMEM((count, d), BF), pltpu.SemaphoreType.DMA((layers, 3))],
        compiler_params=pltpu.CompilerParams(vmem_limit_bytes=VMEM_LIMIT, dimension_semantics=("arbitrary",)),
        name="front",
    )(x, dy, *weights)


def solution(mesh):
    n = mesh.shape["dp"]

    def step(x, dy, *arrays):
        weights, m, v = (arrays[i : i + 3] for i in (0, 3, 6))
        act0, act1, dg1, du1, p0, s0, h1, a0_t, a1_t, dy_t = front(x[0], dy[0], weights)
        return reduce_step_gather(n, dy_t, a1_t, a0_t, act1, dg1, du1, act0, p0, s0, h1, dy[0], weights, m, v)

    rows = P(None, "dp", None)
    return jax.shard_map(
        step,
        mesh=mesh,
        in_specs=(P(("rep", "dp"), None, None),) * 2 + (P(None, None, None),) * 3 + (rows,) * 6,
        out_specs=(P("rep", None, None),) * 3 + (P("rep", "dp", None),) * 6,
        check_vma=False,
    )
```

profile of v0, /device:TPU:96, one launch (start us, length us, event | category | flops | bytes accessed | tf_op | source)
XLA Modules:
  0.0 287.1 jit_solution(9459796308208612298)
XLA Ops:
  0.6 61.2 %front.1 = (bf16[2048,2048]{1,0:T(8,128)(2,1)}, bf16[2048,2048]{1,0:T(8,128)(2,1)}, bf16[2048,2048]{1,0:T(8,128)(2,1)}, bf16[2048,2048]{1,0:T(8,128)(2,1)}, f32[...) custom-call(bf16[2048,640]{1,0:T(8,128)(2,1)} %bitcast.32, ...), custom_call_target="tpu_custom_call" | custom-call | tf_op jit(solution)/shard_map/front/pallas_call | solution.py:563
  61.9 208.9 %reduce_step_gather.1 = (bf16[2,4,4,40,2048]{4,3,2,1,0:T(8,128)(2,1)}, bf16[2,4,4,40,2048]{4,3,2,1,0:T(8,128)(2,1)}, bf16[2,4,4,128,640]{4,3,2,1,0:T(8,128)(2,1)...) custom-call(bf16[640,2048]{1,0:T(8,128)(2,1)} %get-tuple-element.28., ...), custom_call_target="tpu_custom_call" | custom-call | tf_op jit(solution)/shard_map/reduce_step_gather/pallas_call | solution.py:456
  270.8 0.0 copy-start
  270.8 0.0 slice-start
  270.8 6.2 %copy.29 = bf16[2,640,2048]{2,1,0:T(8,128)(2,1)} copy(bf16[2,640,2048]{2,1,0:T(8,128)(2,1)} %bitcast.31) | data formatting | bytes 10485760
  277.0 0.0 copy-done
  277.0 0.0 slice-start.1
  277.0 2.4 copy.30
  279.4 0.0 slice-done
  279.4 0.0 slice-done.1
  279.4 0.0 copy-start.6
  279.4 0.0 copy-start.5
  279.4 0.0 copy-start.4
  279.4 0.0 copy-start.3
  279.4 2.6 copy.31
  282.0 0.0 copy-done.6
  282.1 0.0 copy-start.2
  282.1 0.0 copy-start.1
  282.1 0.8 copy.32
  282.9 0.0 copy-done.5
  282.9 0.8 copy.33
  283.7 0.0 copy-done.4
  283.7 0.8 copy.34
  284.6 0.0 copy-done.3
  284.6 0.8 copy.35
  285.4 0.0 copy-done.2
  285.4 0.8 copy.36
  286.2 0.0 copy-done.1
  286.3 0.8 copy.37
  (1 shorter events, 0.0 us)
Async XLA Ops:
  270.8 6.2 %copy-start = (bf16[2,4,4,40,2048]{4,3,2,1,0:T(8,128)(2,1)S(1)}, bf16[2,4,4,40,2048]{4,3,2,1,0:T(8,128)(2,1)}, u32[]{:S(2)}) copy-start(bf16[2,4,4,40,2048]{4,3,2,1,0:T(8,128)(2,1)} %get-tuple-element.39) | copy-start | bytes 15728644
  270.8 8.5 %slice-start = ((s8[5242880]{0:T(1024)(128)(4,1)}), s8[4194304]{0:T(1024)(128)(4,1)S(1)}, s32[]{:S(2)}) async-start(s8[5242880]{0:T(1024)(128)(4,1)} %bitcast.27), calls=%async_computation | async-start | bytes 8388608
  277.0 2.4 slice-start.1
  279.4 2.7 copy-start.6
  279.4 3.5 %copy-start.5 = (f32[2,40,2048]{2,1,0:T(8,128)S(1)}, f32[2,40,2048]{2,1,0:T(8,128)}, u32[]{:S(2)}) copy-start(f32[2,40,2048]{2,1,0:T(8,128)} %get-tuple-element.60) | copy-start | bytes 1966084
  279.4 4.3 %copy-start.4 = (f32[2,128,640]{2,1,0:T(8,128)S(1)}, f32[2,128,640]{2,1,0:T(8,128)}, u32[]{:S(2)}) copy-start(f32[2,128,640]{2,1,0:T(8,128)} %get-tuple-element.61) | copy-start | bytes 1966084
  279.4 5.2 %copy-start.3 = (f32[2,40,2048]{2,1,0:T(8,128)S(1)}, f32[2,40,2048]{2,1,0:T(8,128)}, u32[]{:S(2)}) copy-start(f32[2,40,2048]{2,1,0:T(8,128)} %get-tuple-element.62) | copy-start | bytes 1966084
  282.1 3.4 %copy-start.2 = (f32[2,40,2048]{2,1,0:T(8,128)S(1)}, f32[2,40,2048]{2,1,0:T(8,128)}, u32[]{:S(2)}) copy-start(f32[2,40,2048]{2,1,0:T(8,128)} %get-tuple-element.63) | copy-start | bytes 1966084
  282.1 4.2 %copy-start.1 = (f32[2,128,640]{2,1,0:T(8,128)S(1)}, f32[2,128,640]{2,1,0:T(8,128)}, u32[]{:S(2)}) copy-start(f32[2,128,640]{2,1,0:T(8,128)} %get-tuple-element.64) | copy-start | bytes 1966084
where the time goes:
time: 288 us; the launch traced here: 287 us
  Pallas kernels  270 us (94%)
  local copies, waits for them, and re-layouts  16.2 us (6%)
    pallas_call x1, Pallas kernels, reduce_step_gather(): pl.pallas_call(functools.partial(step_kernel, side, rows, cols), out_shap...  209 us
    pallas_call x1, Pallas kernels, front(): pl.pallas_call(front_kernel, grid=(TOKEN_BLOCKS,), out_shape=[shape((toke...  61.2 us
    unnamed x27, local copies, waits for them, and re-layouts  16.2 us

commit v1 on v0

--- a/solution.py
+++ b/solution.py
@@ -18,6 +18,24 @@
 TALL = (("d", 1), ("d", 0))
 BLOCKS = 4
 TOKEN_BLOCKS = 4
+FRONT_BLOCKS = 8
+
+ORDER = (
+    ((0, 0),),
+    ((0, 1), (1, 0)),
+    ((0, 2), (1, 1)),
+    ((2, 0), (1, 2)),
+    ((3, 0), (2, 1)),
+    ((4, 0), (3, 1), (2, 2)),
+    ((5, 0), (4, 1), (3, 2)),
+    ((5, 1), (4, 2), (6, 0)),
+    ((5, 2), (6, 1)),
+    (),
+    ((7, 0), (6, 2)),
+    ((0, 3), (8, 0), (7, 1)),
+    ((0, 4), (1, 3), (7, 2)),
+    ((0, 5), (1, 4), (8, 1), (2, 3), (8, 2), (1, 5), (2, 4), (3, 3), (2, 5), (3, 4), (4, 3), (3, 5), (4, 4), (5, 3), (4, 5), (5, 4), (6, 3), (5, 5), (6, 4), (7, 3), (6, 5), (7, 4), (8, 3), (7, 5), (8, 4), (8, 5)),
+)
 
 
 def adamw(w, m, v, g):
@@ -323,11 +341,15 @@
             copy.wait()
 
     def against(buf, slot):
-        total = None
-        for f in range(BLOCKS):
-            term = lax.dot_general(right_buf[slot * TOKEN_BLOCKS + f], buf[:, f * width : (f + 1) * width], (((1,), (1,)), ((), ())), preferred_element_type=F32)
-            total = term if total is None else total + term
-        return total.astype(BF).astype(F32)
+        left = jnp.concatenate([right_buf[slot * TOKEN_BLOCKS + f] for f in range(BLOCKS)], axis=1)
+        return lax.dot_general(left, buf[...], (((1,), (1,)), ((), ())), preferred_element_type=F32).astype(BF).astype(F32)
+
+    def at_block(t, work, part):
+        for k in range(TOKEN_BLOCKS):
+
+            @pl.when(t == k)
+            def _():
+                work(2 * k + part)
 
     def between(work):
         start(tiles(du1, 0, 1))
@@ -364,6 +386,7 @@
             def _():
                 start(state_tiles(t + 1))
 
+            at_block(t, work, 0)
             for f in range(BLOCKS):
                 slot = f % 2
                 if f + 1 < BLOCKS:
@@ -377,12 +400,7 @@
                 start(result_tiles(t, f, slot))
             for f in (BLOCKS - 2, BLOCKS - 1):
                 wait(result_tiles(t, f, f % 2))
-            for k in range(TOKEN_BLOCKS):
-
-                @pl.when(t == k)
-                def _():
-                    work(k)
-
+            at_block(t, work, 1)
             return 0
 
         wait([fill(gate1, 0), fill(up1, 1), down])
@@ -399,12 +417,10 @@
     pl.semaphore_wait(barrier, 4)
 
     stages = (phase1_send, phase1_pass, phase2_send, phase2_pass, update, gather1_pass, gather2_send, gather2_pass, gather2_end)
-    begins = dict(zip(UNITS, (0, 1, 2, 3 + TOKEN_BLOCKS, 4 + TOKEN_BLOCKS, 5 + TOKEN_BLOCKS), strict=True))
 
     def communicate(t):
-        for unit in UNITS:
-            if 0 <= t - begins[unit] < len(stages):
-                stages[t - begins[unit]](unit)
+        for stage, unit in ORDER[t]:
+            stages[stage](UNITS[unit])
 
     d1, g1, u1, d0, g0, u0 = UNITS
     fill(dy_t, 0).wait()
@@ -422,13 +438,12 @@
     fill(a0_t, 0).start()
     right_copy(d0, 0, 0).start()
     gradient(d0, dh_t, g0)
-    communicate(begins[d0])
+    communicate(3 + 2 * TOKEN_BLOCKS)
     fill(a0_t, 0).wait()
     gradient(g0, left_buf.at[0], u0)
-    communicate(begins[g0])
+    communicate(4 + 2 * TOKEN_BLOCKS)
     gradient(u0, left_buf.at[0], None)
-    for t in range(begins[u0], begins[u0] + len(stages)):
-        communicate(t)
+    communicate(5 + 2 * TOKEN_BLOCKS)
     for unit in UNITS:
         wait(result_copies(unit, (1, 2)))
     for src, dst, send, recv, to in sent:
@@ -498,6 +513,10 @@
     return tuple(w.reshape(layers, -1, w.shape[-1]) for w in out[:3]) + tuple(out[3:9])
 
 
+def logistic(x):
+    return 0.5 + 0.5 * jnp.tanh(0.5 * x)
+
+
 def front_kernel(x, dy, *refs):
     weights, (act0, act1, dg1, du1, p0, s0, h1, a0_t, a1_t, dy_t), bufs, a_buf, sem = refs[:3], refs[3:13], refs[13:16], refs[16], refs[17]
     first = pl.program_id(0) == 0
@@ -522,31 +541,32 @@
     normed(x, a0_t)
     dy_t[...] = dy[...].astype(F32).T.astype(BF)
 
-    def ready(layer):
+    def ready(layer, *which):
         @pl.when(first)
         def _():
-            for k in range(3):
+            for k in which:
                 copy(layer, k).wait()
 
-    ready(0)
+    ready(0, 0, 1)
     for f in range(BLOCKS):
         c = slice(f * width, (f + 1) * width)
         gate = jnp.dot(a_buf[...], bufs[0][0, :, c], preferred_element_type=F32)
         up = jnp.dot(a_buf[...], bufs[1][0, :, c], preferred_element_type=F32)
-        sig = jax.nn.sigmoid(gate)
+        sig = logistic(gate)
         silu = gate * sig
         act0[:, c] = (silu * up).astype(BF)
         p0[:, c] = up * (sig + silu * (1 - sig))
         s0[:, c] = silu
+    ready(0, 2)
     h1[...] = (x[...].astype(F32) + jnp.dot(act0[...], bufs[2][0], preferred_element_type=F32).astype(BF).astype(F32)).astype(BF)
     normed(h1, a1_t)
-    ready(1)
+    ready(1, 0, 1, 2)
     for f in range(BLOCKS):
         c = slice(f * width, (f + 1) * width)
         gate = jnp.dot(a_buf[...], bufs[0][1, :, c], preferred_element_type=F32)
         up = jnp.dot(a_buf[...], bufs[1][1, :, c], preferred_element_type=F32)
         d = lax.dot_general(dy[...], bufs[2][1, c, :], (((1,), (1,)), ((), ())), preferred_element_type=F32).astype(BF).astype(F32)
-        sig = jax.nn.sigmoid(gate)
+        sig = logistic(gate)
         silu = gate * sig
         act1[:, c] = (silu * up).astype(BF)
         dg1[:, c] = (d * up * (sig + silu * (1 - sig))).astype(BF)
@@ -556,13 +576,13 @@
 def front(x, dy, weights):
     tokens, d = x.shape
     layers, _, ff = weights[0].shape
-    count = tokens // TOKEN_BLOCKS
+    count = tokens // FRONT_BLOCKS
     row = lambda n: pl.BlockSpec((count, n), lambda t: (t, 0))
     column = pl.BlockSpec((d, count), lambda t: (0, t))
     shape = jax.ShapeDtypeStruct
     return pl.pallas_call(
         front_kernel,
-        grid=(TOKEN_BLOCKS,),
+        grid=(FRONT_BLOCKS,),
         out_shape=[shape((tokens, ff), BF)] * 4 + [shape((tokens, ff), F32)] * 2 + [shape((tokens, d), BF)] + [shape((d, tokens), BF)] * 3,
         in_specs=[row(d)] * 2 + [ANY] * 3,
         out_specs=[row(ff)] * 6 + [row(d)] + [column] * 3,

time: 288 us -> 263 us (0.913)
  Pallas kernels: 270 us -> 246 us
    pallas_call x1, Pallas kernels: 209 us -> 187 us  [reduce_step_gather(): pl.pallas_call(functools.partial(step_kernel, side, rows, cols), out_shap...]
where the time goes in v1:
time: 263 us
  Pallas kernels  246 us (94%)
  local copies, waits for them, and re-layouts  16.2 us (6%)
    pallas_call x1, Pallas kernels, reduce_step_gather(): pl.pallas_call(functools.partial(step_kernel, side, rows, cols), out_shap...  187 us
    pallas_call x1, Pallas kernels, front(): pl.pallas_call(front_kernel, grid=(FRONT_BLOCKS,), out_shape=[shape((toke...  58.5 us
    unnamed x27, local copies, waits for them, and re-layouts  16.2 us

profile of v1, /device:TPU:96, one launch (start us, length us, event | category | flops | bytes accessed | tf_op | source)
XLA Modules:
  0.0 262.7 jit_solution(345264535816846474)
XLA Ops:
  0.6 58.5 %front.1 = (bf16[2048,2048]{1,0:T(8,128)(2,1)}, bf16[2048,2048]{1,0:T(8,128)(2,1)}, bf16[2048,2048]{1,0:T(8,128)(2,1)}, bf16[2048,2048]{1,0:T(8,128)(2,1)}, f32[...) custom-call(bf16[2048,640]{1,0:T(8,128)(2,1)} %bitcast.32, ...), custom_call_target="tpu_custom_call" | custom-call | tf_op jit(solution)/shard_map/front/pallas_call | solution.py:583
  59.2 187.2 %reduce_step_gather.1 = (bf16[2,4,4,40,2048]{4,3,2,1,0:T(8,128)(2,1)}, bf16[2,4,4,40,2048]{4,3,2,1,0:T(8,128)(2,1)}, bf16[2,4,4,128,640]{4,3,2,1,0:T(8,128)(2,1)...) custom-call(bf16[640,2048]{1,0:T(8,128)(2,1)} %get-tuple-element.28., ...), custom_call_target="tpu_custom_call" | custom-call | tf_op jit(solution)/shard_map/reduce_step_gather/pallas_call | solution.py:471
  246.4 0.0 copy-start
  246.4 0.0 slice-start
  246.4 6.2 %copy.29 = bf16[2,640,2048]{2,1,0:T(8,128)(2,1)} copy(bf16[2,640,2048]{2,1,0:T(8,128)(2,1)} %bitcast.31) | data formatting | bytes 10485760
  252.6 0.0 copy-done
  252.6 0.0 slice-start.1
  252.6 2.4 copy.30
  254.9 0.0 slice-done
  254.9 0.0 slice-done.1
  254.9 0.0 copy-start.6
  254.9 0.0 copy-start.5
  254.9 0.0 copy-start.4
  255.0 0.0 copy-start.3
  255.0 2.6 %copy.31 = bf16[2,2048,640]{2,1,0:T(8,128)(2,1)} copy(bf16[2,2048,640]{2,1,0:T(8,128)(2,1)S(1)} %bitcast.29) | data formatting | bytes 10485760
  257.6 0.0 copy-done.6
  257.6 0.0 copy-start.2
  257.6 0.0 copy-start.1
  257.6 0.8 copy.32
  258.5 0.0 copy-done.5
  258.5 0.8 copy.33
  259.3 0.0 copy-done.4
  259.3 0.8 copy.34
  260.1 0.0 copy-done.3
  260.1 0.8 copy.35
  261.0 0.0 copy-done.2
  261.0 0.8 copy.36
  261.8 0.0 copy-done.1
  261.8 0.8 copy.37
  (1 shorter events, 0.0 us)
Async XLA Ops:
  246.4 6.2 %copy-start = (bf16[2,4,4,40,2048]{4,3,2,1,0:T(8,128)(2,1)S(1)}, bf16[2,4,4,40,2048]{4,3,2,1,0:T(8,128)(2,1)}, u32[]{:S(2)}) copy-start(bf16[2,4,4,40,2048]{4,3,2,1,0:T(8,128)(2,1)} %get-tuple-element.39) | copy-start | bytes 15728644
  246.4 8.5 %slice-start = ((s8[5242880]{0:T(1024)(128)(4,1)}), s8[4194304]{0:T(1024)(128)(4,1)S(1)}, s32[]{:S(2)}) async-start(s8[5242880]{0:T(1024)(128)(4,1)} %bitcast.27), calls=%async_computation | async-start | bytes 8388608
  252.6 2.4 slice-start.1
  254.9 2.7 %copy-start.6 = (f32[2,40,2048]{2,1,0:T(8,128)S(1)}, f32[2,40,2048]{2,1,0:T(8,128)}, u32[]{:S(2)}) copy-start(f32[2,40,2048]{2,1,0:T(8,128)} %get-tuple-element.59) | copy-start | bytes 1966084
  254.9 3.5 %copy-start.5 = (f32[2,40,2048]{2,1,0:T(8,128)S(1)}, f32[2,40,2048]{2,1,0:T(8,128)}, u32[]{:S(2)}) copy-start(f32[2,40,2048]{2,1,0:T(8,128)} %get-tuple-element.60) | copy-start | bytes 1966084
  254.9 4.3 %copy-start.4 = (f32[2,128,640]{2,1,0:T(8,128)S(1)}, f32[2,128,640]{2,1,0:T(8,128)}, u32[]{:S(2)}) copy-start(f32[2,128,640]{2,1,0:T(8,128)} %get-tuple-element.61) | copy-start | bytes 1966084
  255.0 5.2 %copy-start.3 = (f32[2,40,2048]{2,1,0:T(8,128)S(1)}, f32[2,40,2048]{2,1,0:T(8,128)}, u32[]{:S(2)}) copy-start(f32[2,40,2048]{2,1,0:T(8,128)} %get-tuple-element.62) | copy-start | bytes 1966084
  257.6 3.4 %copy-start.2 = (f32[2,40,2048]{2,1,0:T(8,128)S(1)}, f32[2,40,2048]{2,1,0:T(8,128)}, u32[]{:S(2)}) copy-start(f32[2,40,2048]{2,1,0:T(8,128)} %get-tuple-element.63) | copy-start | bytes 1966084
  257.6 4.2 %copy-start.1 = (f32[2,128,640]{2,1,0:T(8,128)S(1)}, f32[2,128,640]{2,1,0:T(8,128)}, u32[]{:S(2)}) copy-start(f32[2,128,640]{2,1,0:T(8,128)} %get-tuple-element.64) | copy-start | bytes 1966084
